TPU v7x, 32 devices: a whole 2x2x4 slice. The times are simulated.
32 devices in a mesh: clip: 4 (over z), tm: 8 (over y, x, core).
Axes of the slice: x: 2, y: 2, z: 4, core: 2. Of those that a mesh axis runs over, the one named last changes fastest.
Arguments:
- tokens: bfloat16 [4, 8, 256, 2048], P('clip', 'tm'), may hold values from -16 to 16
- spatial_queries: bfloat16 [4, 8, 256, 1024], P('clip', 'tm'), may hold values from -4.5 to 4.5
- spatial_keys: bfloat16 [4, 8, 256, 1024], P('clip', 'tm'), may hold values from -4.5 to 4.5
- spatial_values: bfloat16 [4, 8, 256, 1024], P('clip', 'tm'), may hold values from -6 to 6
- spatial_proj: bfloat16 [1024, 2048], P('tm'), may hold values from -0.1875 to 0.1875
- temporal_qkv: bfloat16 [2048, 3072], P('tm'), may hold values from -0.13258252 to 0.13258252
- temporal_proj: bfloat16 [1024, 2048], P('tm'), may hold values from -0.1875 to 0.1875
- frame_mask: int32 [4, 8, 8], P('clip'), may hold values from 0 to 1, as said below
- expert_ids: int32 [4, 8, 256, 2], P('clip', 'tm'), may hold values from 0 to 31, all different within a row; in each aligned block of 256 rows (0 to 255, 256 to 511, ..., all dimensions but the last counted through in order) at most 32 rows name the same one
- gate_values: float32 [4, 8, 256, 2], P('clip', 'tm'), may hold values from 0.2 to 1
- expert_gate: bfloat16 [32, 2048, 1408], P(('clip', 'tm')), may hold values from -0.125 to 0.125
- expert_up: bfloat16 [32, 2048, 1408], P(('clip', 'tm')), may hold values from -0.125 to 0.125
- expert_down: bfloat16 [32, 1408, 2048], P(('clip', 'tm')), may hold values from -0.15625 to 0.15625
Outputs:
- layer_out: bfloat16 [4, 8, 256, 2048], P('clip', 'tm')
Inputs may be any that keep to these rules, and one draw needn't show every extreme that they name: `expert_ids`: each token names 2 different experts. Among the 256 tokens of one clip and frame, no expert is named by more than 32 tokens, and in some frames one expert is named by exactly 32. frame_mask[c, i, j] is 1 where j = i and 0 where j > i.
All inputs are finite; a program needn't handle non-finite values.
Results may differ from a plain program's by a relative error of at most 0.013.
Values may be sent and summed in bfloat16 or wider, within the bound.
No kernel may reach another device: no remote copies, remote signals or barrier semaphores. Data moves between devices by JAX's collectives and lax.ppermute only.
A program may use at most 128 MiB of HBM per device.

v0:
```python
import math

import jax
import jax.numpy as jnp
from jax import lax
from jax.sharding import PartitionSpec as P

HEADS = 8
HD = 128
TOP = 2


EPS = 1e-06
MASKED = -1e30


def rms_normed(values):
    wide = values.astype(jnp.float32)
    inverse = lax.rsqrt(jnp.mean(wide * wide, axis=-1, keepdims=True) + EPS)
    return (wide * inverse).astype(jnp.bfloat16)


def normalize_rows(scores):
    row_max = jnp.max(scores, axis=-1, keepdims=True)
    exp_terms = jnp.exp(scores - row_max)
    return (exp_terms / jnp.sum(exp_terms, axis=-1, keepdims=True)).astype(jnp.bfloat16)


def add_columns(left_side, piece):
    return jnp.dot(left_side, piece, preferred_element_type=jnp.float32)


def spatial_mix(queries, keys, values):
    positions = queries.shape[0]
    score_scale = 1.0 / math.sqrt(HD)
    query_heads = queries.reshape(positions, HEADS, HD)
    key_heads = keys.reshape(positions, HEADS, HD)
    value_heads = values.reshape(positions, HEADS, HD)
    scores = (
        jnp.einsum("qhd,khd->hqk", query_heads, key_heads, preferred_element_type=jnp.float32)
        * score_scale
    )
    weights = normalize_rows(scores)
    mixed = jnp.einsum("hqk,khd->qhd", weights, value_heads, preferred_element_type=jnp.float32)
    return mixed.astype(jnp.bfloat16).reshape(positions, HEADS * HD)


def temporal_mix(queries, keys, values, allowed):
    frames, positions = (queries.shape[0], queries.shape[1])
    score_scale = 1.0 / math.sqrt(HD)
    query_heads = queries.reshape(frames, positions, HEADS, HD)
    key_heads = keys.reshape(frames, positions, HEADS, HD)
    value_heads = values.reshape(frames, positions, HEADS, HD)
    scores = (
        jnp.einsum("iphd,jphd->phij", query_heads, key_heads, preferred_element_type=jnp.float32)
        * score_scale
    )
    weights = normalize_rows(jnp.where(allowed[None, None, :, :], scores, MASKED))
    mixed = jnp.einsum("phij,jphd->iphd", weights, value_heads, preferred_element_type=jnp.float32)
    return mixed.astype(jnp.bfloat16).reshape(frames, positions, HEADS * HD)


def temporal_inputs(normed, qkv_rows):
    zero_start = jnp.zeros((normed.shape[0], qkv_rows.shape[1]), jnp.float32)

    def fold_rows(total, piece, start):
        return add_columns(normed, piece)

    return fold_rows(
        zero_start, lax.all_gather(qkv_rows, "tm", axis=0, tiled=True), jnp.int32(0)
    ).astype(jnp.bfloat16)


def temporal_output(mixed, proj_rows):
    zero_start = jnp.zeros((mixed.shape[0], proj_rows.shape[1]), jnp.float32)

    def fold_rows(total, piece, start):
        return add_columns(mixed, piece)

    return fold_rows(
        zero_start, lax.all_gather(proj_rows, "tm", axis=0, tiled=True), jnp.int32(0)
    ).astype(jnp.bfloat16)


def shards(
    tokens,
    spatial_queries,
    spatial_keys,
    spatial_values,
    spatial_proj,
    temporal_qkv,
    temporal_proj,
    frame_mask,
    expert_ids,
    gate_values,
    expert_gate,
    expert_up,
    expert_down,
):
    model_width = tokens.shape[3]
    positions = tokens.shape[2]
    tm_count = lax.axis_size("tm")
    clip_count = lax.axis_size("clip")
    experts = clip_count * tm_count
    per_block = positions // tm_count
    resident = tokens.reshape(positions, model_width)
    attended_space = spatial_mix(
        spatial_queries.reshape(positions, -1),
        spatial_keys.reshape(positions, -1),
        spatial_values.reshape(positions, -1),
    )
    spatial_update = add_columns(
        attended_space, lax.all_gather(spatial_proj, "tm", axis=0, tiled=True)
    )
    first = (resident.astype(jnp.float32) + spatial_update).astype(jnp.bfloat16)
    normed = rms_normed(first)
    allowed = frame_mask[0] == 1
    by_position = lax.all_to_all(
        normed.reshape(tm_count, per_block, model_width),
        "tm",
        split_axis=0,
        concat_axis=0,
        tiled=True,
    )
    frames = by_position.shape[0]
    projected = temporal_inputs(by_position.reshape(frames * per_block, model_width), temporal_qkv)
    head_width = projected.shape[1] // 3
    triple = projected.reshape(frames, per_block, 3 * head_width)
    attended_time = temporal_mix(
        triple[:, :, :head_width],
        triple[:, :, head_width : 2 * head_width],
        triple[:, :, 2 * head_width :],
        allowed,
    )
    update_rows = temporal_output(
        attended_time.reshape(frames * per_block, head_width), temporal_proj
    )
    returned = lax.all_to_all(
        update_rows.reshape(frames, per_block, model_width),
        "tm",
        split_axis=0,
        concat_axis=0,
        tiled=True,
    )
    temporal_update = returned.reshape(positions, model_width)
    second = (first.astype(jnp.float32) + temporal_update.astype(jnp.float32)).astype(jnp.bfloat16)
    routed = rms_normed(second)
    capacity = 2 * TOP * positions // experts
    slot_count = experts * capacity
    pair_ids = expert_ids.reshape(positions * TOP)
    chosen = (pair_ids[:, None] == jnp.arange(experts, dtype=jnp.int32)[None, :]).astype(jnp.int32)
    earlier = jnp.cumsum(chosen, axis=0) - chosen
    pair_rank = jnp.sum(earlier * chosen, axis=1)
    pair_slot = pair_ids * capacity + pair_rank
    slot_index = jnp.arange(slot_count, dtype=jnp.int32)
    pair_onehot = (pair_slot[:, None] == slot_index[None, :]).astype(jnp.bfloat16)
    token_onehot = jnp.any(
        pair_slot.reshape(positions, TOP)[:, :, None] == slot_index[None, None, :], axis=1
    ).astype(jnp.bfloat16)
    outgoing = lax.dot_general(
        token_onehot, routed, (((0,), (0,)), ((), ())), preferred_element_type=jnp.float32
    )
    outgoing = outgoing.astype(jnp.bfloat16).reshape(experts, capacity, model_width)
    received = lax.all_to_all(outgoing, ("clip", "tm"), split_axis=0, concat_axis=0, tiled=True)
    flat_rows = received.reshape(-1, model_width)
    gate_part = jnp.dot(flat_rows, expert_gate[0], preferred_element_type=jnp.float32)
    up_part = jnp.dot(flat_rows, expert_up[0], preferred_element_type=jnp.float32)
    hidden = (jax.nn.silu(gate_part) * up_part).astype(jnp.bfloat16)
    answer = jnp.dot(hidden, expert_down[0], preferred_element_type=jnp.float32).astype(
        jnp.bfloat16
    )
    answers = lax.all_to_all(
        answer.reshape(received.shape), ("clip", "tm"), split_axis=0, concat_axis=0, tiled=True
    )
    pair_answers = jnp.dot(
        pair_onehot, answers.reshape(slot_count, model_width), preferred_element_type=jnp.float32
    )
    weighted = pair_answers.reshape(positions, TOP, model_width) * gate_values.reshape(
        positions, TOP, 1
    )
    expert_mix = jnp.sum(weighted, axis=1)
    layer_out = (second.astype(jnp.float32) + expert_mix).astype(jnp.bfloat16)
    return layer_out.reshape(tokens.shape)


def solution(mesh):
    placed = (
        P("clip", "tm", None, None),
        P("clip", "tm", None, None),
        P("clip", "tm", None, None),
        P("clip", "tm", None, None),
        P("tm", None),
        P("tm", None),
        P("tm", None),
        P("clip", None, None),
        P("clip", "tm", None, None),
        P("clip", "tm", None, None),
        P(("clip", "tm"), None, None),
        P(("clip", "tm"), None, None),
        P(("clip", "tm"), None, None),
    )
    return jax.shard_map(
        shards, mesh=mesh, in_specs=placed, out_specs=P("clip", "tm", None, None), check_vma=False
    )
```

profile of v0, /device:TPU:0, one launch (start us, length us, event | category | flops | bytes accessed | tf_op | source)
XLA Modules:
  0.0 431.3 jit_solution(4802736948756652451)
XLA Ops:
  6.5 0.7 all-gather.4.cloned.1.call-update
  7.3 0.7 all-gather.6.cloned.1.call-update
  8.1 0.7 all-gather.8.cloned.1.call-update
  8.7 1.1 copy.56
  9.9 1.1 copy.57
  11.2 2.1 fusion.71
  13.4 2.0 convolution_convert_fusion.4
  15.4 33.2 %all-gather.4.cloned.1.call-done = bf16[1024,2048]{1,0:T(8,128)(2,1)} async-done(((bf16[128,2048]{1,0:T(8,128)(2,1)}), bf16[1024,2048]{1,0:T(8,128)(2,1)}) %all-gather.4.cloned.1.call-update) | async-done | bytes 4194320 | tf_op jit(solution)/shard_map/all_gather | solution.py:113
  48.6 3.6 fusion.19
  52.2 1.2 fusion.20
  53.4 3.6 all-to-all-start
  57.1 25.5 %all-to-all-done = bf16[8,32,2048]{2,1,0:T(8,128)(2,1)S(1)} async-done(((bf16[8,32,2048]{2,1,0:T(8,128)(2,1)}), bf16[8,32,2048]{2,1,0:T(8,128)(2,1)S(1)}, u32[]{:S(2)}, u32[]{:S(2)}) %all-to-all-start) | async-done | bytes 1048608 | tf_op jit(solution)/shard_map/all_to_all | solution.py:118
  82.6 49.2 %all-gather.6.cloned.1.call-done = bf16[2048,3072]{1,0:T(8,128)(2,1)} async-done(((bf16[256,3072]{1,0:T(8,128)(2,1)}), bf16[2048,3072]{1,0:T(8,128)(2,1)}) %all-gather.6.cloned.1.call-update) | async-done | bytes 12582928 | tf_op jit(solution)/shard_map/all_gather | solution.py:70
  131.8 8.0 %convolution_convert_fusion = bf16[256,3072]{1,0:T(8,128)(2,1)S(1)} fusion(bf16[256,2048]{1,0:T(8,128)(2,1)S(1)} %bitcast.117, bf16[2048,3072]{1,0:T(8,128)(2,1)} %all-gather.6.cloned.1.call-done), kind=kOutput, calls=%fused_computation.10 | convolution fusion | flops 3222011904 | bytes 15204352 | tf_op jit(solution)/shard_map/dot_general | solution.py:30
  140.3 2.1 fusion.76
  142.4 1.8 fusion.32
  144.3 26.0 %all-gather.8.cloned.1.call-done = bf16[1024,2048]{1,0:T(8,128)(2,1)} async-done(((bf16[128,2048]{1,0:T(8,128)(2,1)}), bf16[1024,2048]{1,0:T(8,128)(2,1)}) %all-gather.8.cloned.1.call-update) | async-done | bytes 4194320 | tf_op jit(solution)/shard_map/all_gather | solution.py:81
  170.3 4.4 %convolution_convert_fusion.2 = bf16[256,2048]{1,0:T(8,128)(2,1)} fusion(bf16[1024,2048]{1,0:T(8,128)(2,1)} %all-gather.8.cloned.1.call-done, bf16[32,8,8,128]{3,2,1,0:T(8,128)(2,1)S(1)} %bitcast.124), kind=kOutput, calls=%fused_computation.22 | convolution fusion | flops 1074266112 | bytes 5767168 | tf_op jit(solution)/shard_map/dot_general | solution.py:30
  174.7 3.7 all-to-all-start.1
  178.9 1.2 reduce-window.6
  180.1 0.2 slice_reduce_fusion
  180.7 0.3 fusion.27
  181.0 12.6 %all-to-all-done.1 = bf16[8,32,2048]{2,1,0:T(8,128)(2,1)S(1)} async-done(((bf16[8,32,2048]{2,1,0:T(8,128)(2,1)}), bf16[8,32,2048]{2,1,0:T(8,128)(2,1)S(1)}, u32[]{:S(2)}, u32[]{:S(2)}) %all-to-all-start.1) | async-done | bytes 1048608 | tf_op jit(solution)/shard_map/all_to_all | solution.py:138
  193.6 0.5 fusion.22
  194.2 1.4 convolution_convert_fusion.1
  195.6 97.1 %all_to_all.20 = bf16[32,32,2048]{2,1,0:T(8,128)(2,1)S(1)} all-to-all(bf16[32,32,2048]{2,1,0:T(8,128)(2,1)S(1)} %bitcast.108), channel_id=1, replica_groups=mesh['clip'=4,'tm'=8] {'clip','tm'}, dimensions={0} | all-to-all | bytes 8388608 | tf_op jit(solution)/shard_map/all_to_all | solution.py:164
  292.7 2.0 copy-done
  294.7 8.4 %fusion.6 = f32[1024,1408]{1,0:T(8,128)} fusion(bf16[1024,2048]{1,0:T(8,128)(2,1)S(1)} %bitcast.109, bf16[1,2048,1408]{2,1,0:T(8,128)(2,1)S(1)} %bitcast.128), kind=kOutput, calls=%fused_computation.6 | convolution fusion | flops 5905580032 | bytes 15728640 | tf_op jit(solution)/shard_map/dot_general | solution.py:166
  303.2 20.6 %fusion.12 = bf16[1024,2048]{1,0:T(8,128)(2,1)} fusion(bf16[1,1408,2048]{2,1,0:T(8,128)(2,1)} %param.25, f32[1024,1408]{1,0:T(8,128)} %fusion.6, bf16[1024,2048]{1,0:T(8,128)(2,1)} %bitcast.110, bf16[1,2048,1408]{2,1,0:T(8,128)(2,1)} %param.24), kind=kOutput, calls=%fused_computation.12 | convolution fusion | flops 11821907968 | bytes 25690112 | tf_op jit(solution)/shard_map/dot_general | solution.py:169
  323.8 97.3 %all_to_all.21 = bf16[32,32,2048]{2,1,0:T(8,128)(2,1)S(1)} all-to-all(bf16[32,32,2048]{2,1,0:T(8,128)(2,1)} %bitcast.111), channel_id=1, replica_groups=mesh['clip'=4,'tm'=8] {'clip','tm'}, dimensions={0} | all-to-all | bytes 8388608 | tf_op jit(solution)/shard_map/all_to_all | solution.py:172
  421.1 2.4 multiply_reduce_fusion
  423.5 1.3 fusion.33
  (39 shorter events, 1.8 us)
Async XLA Ops:
  6.5 4.5 %copy-start.1 = (bf16[1,1,256,1024]{3,2,1,0:T(8,128)(2,1)S(1)}, bf16[1,1,256,1024]{3,2,1,0:T(8,128)(2,1)}, u32[]{:S(2)}) copy-start(bf16[1,1,256,1024]{3,2,1,0:T(8,128)(2,1)} %param.16) | copy-start | bytes 1572868
  6.5 42.0 %all-gather.4.cloned.1.call-start = ((), (), s32[]{:S(2)}) async-start(), calls=%async_computation.4 | async-start | bytes 4718592 | tf_op jit(solution)/shard_map/all_gather | solution.py:113
  7.3 124.5 %all-gather.6.cloned.1.call-start = ((), (), s32[]{:S(2)}) async-start(), calls=%async_computation.5 | async-start | bytes 14155776 | tf_op jit(solution)/shard_map/all_gather | solution.py:70
  8.0 162.3 %all-gather.8.cloned.1.call-start = ((), (), s32[]{:S(2)}) async-start(), calls=%async_computation.6 | async-start | bytes 4718592 | tf_op jit(solution)/shard_map/all_gather | solution.py:81
  13.4 35.2 %copy-start.4 = (bf16[1,1,256,2048]{3,2,1,0:T(8,128)(2,1)S(1)}, bf16[1,1,256,2048]{3,2,1,0:T(8,128)(2,1)}, u32[]{:S(2)}) copy-start(bf16[1,1,256,2048]{3,2,1,0:T(8,128)(2,1)} %param.13) | copy-start | bytes 3145732
  48.6 8.4 %copy-start.2 = (s32[1,8,8]{2,1,0:T(8,128)S(1)}, s32[1,8,8]{2,1,0:T(8,128)}, u32[]{:S(2)}) copy-start(s32[1,8,8]{2,1,0:T(8,128)} %param.20) | copy-start | bytes 772
  53.4 29.2 %all-to-all-start = ((bf16[8,32,2048]{2,1,0:T(8,128)(2,1)}), bf16[8,32,2048]{2,1,0:T(8,128)(2,1)S(1)}, u32[]{:S(2)}, u32[]{:S(2)}) async-start(bf16[8,32,2048]{2,1,0:T(8,128)(2,1)} %bitcast.4), calls=%async_computation | async-start | bytes 2097152 | tf_op jit(solution)/shard_map/all_to_all | solution.py:118
  170.3 8.2 %copy-start.3 = (s32[1,1,256,2]{2,3,1,0:T(2,128)S(1)}, s32[1,1,256,2]{2,3,1,0:T(2,128)}, u32[]{:S(2)}) copy-start(s32[1,1,256,2]{2,3,1,0:T(2,128)} %param.21) | copy-start | bytes 6148
  174.7 18.9 %all-to-all-start.1 = ((bf16[8,32,2048]{2,1,0:T(8,128)(2,1)}), bf16[8,32,2048]{2,1,0:T(8,128)(2,1)S(1)}, u32[]{:S(2)}, u32[]{:S(2)}) async-start(bf16[8,32,2048]{2,1,0:T(8,128)(2,1)} %bitcast.9), calls=%async_computation.1 | async-start | bytes 2097152 | tf_op jit(solution)/shard_map/all_to_all | solution.py:138
  193.6 101.1 %slice-start = ((s8[5767168]{0:T(1024)(128)(4,1)}), s8[4194304]{0:T(1024)(128)(4,1)S(1)}, s32[]{:S(2)}) async-start(s8[5767168]{0:T(1024)(128)(4,1)} %bitcast.127), calls=%async_computation.7 | async-start | bytes 8388608
  194.2 100.6 %slice-start.1 = ((s8[5767168]{0:T(1024)(128)(4,1)}), s8[1572864]{0:T(1024)(128)(4,1)S(1)}, s32[]{:S(2)}) async-start(s8[5767168]{0:T(1024)(128)(4,1)} %bitcast.127), calls=%async_computation.8 | async-start | bytes 3145728
  292.7 2.0 copy-start
  323.8 97.3 %copy-start.5 = (f32[1,1,256,2]{2,3,1,0:T(2,128)S(1)}, f32[1,1,256,2]{2,3,1,0:T(2,128)}, u32[]{:S(2)}) copy-start(f32[1,1,256,2]{2,3,1,0:T(2,128)} %param.22) | copy-start | bytes 6148
Sparse Core Ops, SparseCore 0:
  9.2 39.2 all-gather.3
  50.4 81.2 all-gather.5
  133.7 36.5 all-gather.7
where the time goes:
time: 432 us; the launch traced here: 431 us
  blocking collectives  194 us (45%)
  waiting for transfers between devices  149 us (34%)
  matrix products  57 us (13%)
  between operations  13.3 us (3%)
  starting transfers between devices  7.38 us (2%)
  local copies, waits for them, and re-layouts  5.99 us (1%)
  other arithmetic  4.69 us (1%)
    all_to_all x1, blocking collectives, shards(): lax.all_to_all(answer.reshape(received.shape), ('clip', 'tm'), split_axis...  97.3 us
    all_to_all x1, blocking collectives, shards(): lax.all_to_all(outgoing, ('clip', 'tm'), split_axis=0, concat_axis=0, til...  97.1 us
    all_gather x1, waiting for transfers between devices, temporal_inputs(): lax.all_gather(qkv_rows, 'tm', axis=0, tiled=True)  49.2 us
    all_gather x1, waiting for transfers between devices, shards(): lax.all_gather(spatial_proj, 'tm', axis=0, tiled=True)  33.2 us
    all_gather x1, waiting for transfers between devices, temporal_output(): lax.all_gather(proj_rows, 'tm', axis=0, tiled=True)  26 us
    all_to_all x1, waiting for transfers between devices, shards(): lax.all_to_all(normed.reshape(tm_count, per_block, model_width), 'tm', sp...  25.5 us
    dot_general x1, matrix products, shards(): jnp.dot(hidden, expert_down[0], preferred_element_type=jnp.float32)  20.6 us
    dot_general x3, matrix products, add_columns(): return jnp.dot(left_side, piece, preferred_element_type=jnp.float32)  16.1 us
  transfers between devices with their start and end apart: 5, of which 5 were waited for; matrix products, arithmetic and copies ran while one was open for 6% of the time, Pallas kernels for 0%

commit v1 on v0

v1 whole, which is shorter than its diff:
```python
import math

import jax
import jax.numpy as jnp
from jax import lax
from jax.experimental import pallas as pl
from jax.experimental.pallas import tpu as pltpu
from jax.sharding import PartitionSpec as P


HEADS = 8
HD = 128
TOP = 2


EPS = 1e-06
MASKED = -1e30


def rms_normed(values):
    wide = values.astype(jnp.float32)
    inverse = lax.rsqrt(jnp.mean(wide * wide, axis=-1, keepdims=True) + EPS)
    return (wide * inverse).astype(jnp.bfloat16)


def normalize_rows(scores):
    row_max = jnp.max(scores, axis=-1, keepdims=True)
    exp_terms = jnp.exp(scores - row_max)
    return (exp_terms / jnp.sum(exp_terms, axis=-1, keepdims=True)).astype(jnp.bfloat16)


def add_columns(left_side, piece):
    return jnp.dot(left_side, piece, preferred_element_type=jnp.float32)


def spatial_mix(queries, keys, values):
    positions = queries.shape[0]
    score_scale = 1.0 / math.sqrt(HD)
    query_heads = queries.reshape(positions, HEADS, HD)
    key_heads = keys.reshape(positions, HEADS, HD)
    value_heads = values.reshape(positions, HEADS, HD)
    scores = (
        jnp.einsum("qhd,khd->hqk", query_heads, key_heads, preferred_element_type=jnp.float32)
        * score_scale
    )
    weights = normalize_rows(scores)
    mixed = jnp.einsum("hqk,khd->qhd", weights, value_heads, preferred_element_type=jnp.float32)
    return mixed.astype(jnp.bfloat16).reshape(positions, HEADS * HD)


def temporal_mix(queries, keys, values, allowed):
    frames, positions = (queries.shape[0], queries.shape[1])
    score_scale = 1.0 / math.sqrt(HD)
    query_heads = queries.reshape(frames, positions, HEADS, HD)
    key_heads = keys.reshape(frames, positions, HEADS, HD)
    value_heads = values.reshape(frames, positions, HEADS, HD)
    scores = (
        jnp.einsum("iphd,jphd->phij", query_heads, key_heads, preferred_element_type=jnp.float32)
        * score_scale
    )
    weights = normalize_rows(jnp.where(allowed[None, None, :, :], scores, MASKED))
    mixed = jnp.einsum("phij,jphd->iphd", weights, value_heads, preferred_element_type=jnp.float32)
    return mixed.astype(jnp.bfloat16).reshape(frames, positions, HEADS * HD)


def after(value, *earlier):
    return lax.optimization_barrier((value, *earlier))[0]


def swapped(piece, bit):
    count = lax.axis_size("tm")
    return lax.ppermute(piece, "tm", [(i, i ^ bit) for i in range(count)])


def high_bits():
    count = lax.axis_size("tm")
    return (count // 2, count // 4)


def direct_piece(rows, place):
    return swapped(rows, high_bits()[place])


def far_piece(held, route):
    return swapped(held, high_bits()[1 - route])


def partner_pieces(pieces):
    count = lax.axis_size("clip")
    return [
        lax.ppermute(piece, "clip", [(i, i ^ 1) for i in range(count)]) for piece in pieces
    ]


def all_pieces(rows, direct, far, earlier=()):
    high, low = high_bits()
    pieces = [(0, rows), (high, direct[0]), (low, direct[1]), (high | low, far)]
    bit = low // 2
    while bit:
        pieces = pieces + [
            (offset | bit, swapped(after(piece, *earlier) if earlier else piece, bit))
            for offset, piece in pieces
        ]
        bit //= 2
    return pieces


def times_rows(left_side, pieces, added=None):
    here = lax.axis_index("tm")
    height, width = pieces[0][1].shape
    places = jnp.stack([here ^ offset for offset, _ in pieces]).astype(jnp.int32)
    if height % 128:
        total = None if added is None else added.astype(jnp.float32)
        for number, (_, piece) in enumerate(pieces):
            columns = lax.dynamic_slice_in_dim(left_side, places[number] * height, height, axis=1)
            product = add_columns(columns, piece)
            total = product if total is None else total + product
        total = total.astype(jnp.bfloat16)
        return total if added is None else (total, rms_normed(total))
    extra = [] if added is None else [added]

    def body(places_ref, left_ref, *refs):
        out_refs = refs[len(pieces) + len(extra) :]
        total = None
        for number in range(len(pieces)):
            start = pl.multiple_of(places_ref[number] * height, 128)
            product = jnp.dot(
                left_ref[:, pl.ds(start, height)],
                refs[number][...],
                preferred_element_type=jnp.float32,
            )
            total = product if total is None else total + product
        if extra:
            total = total + refs[len(pieces)][...].astype(jnp.float32)
        rounded = total.astype(jnp.bfloat16)
        out_refs[0][...] = rounded
        if extra:
            out_refs[1][...] = rms_normed(rounded)

    out = jax.ShapeDtypeStruct((left_side.shape[0], width), jnp.bfloat16)
    whole = pl.BlockSpec(memory_space=pltpu.VMEM)
    return pl.pallas_call(
        body,
        out_shape=[out, out] if extra else out,
        in_specs=[pl.BlockSpec(memory_space=pltpu.SMEM)]
        + [whole] * (1 + len(pieces) + len(extra)),
        out_specs=[whole, whole] if extra else whole,
        name="times_rows",
    )(places, left_side, *[piece for _, piece in pieces], *extra)


def expert_rows(blocks, gate, up, down):
    count, model_width = blocks[0].shape
    rows = count * len(blocks)
    width = 512
    while model_width % width:
        width //= 2
    steps = model_width // width
    number = len(blocks)

    def body(*refs):
        ins, (gate_ref, up_ref, down_ref) = refs[:number], refs[number : number + 3]
        outs = refs[number + 3 : 2 * number + 3]
        gate_here, up_here, down_here, all_rows, arrived = refs[2 * number + 3 :]

        def copies(step):
            span = pl.ds(step * width, width)
            return [
                pltpu.make_async_copy(gate_ref.at[span], gate_here.at[span], arrived.at[0, step]),
                pltpu.make_async_copy(up_ref.at[span], up_here.at[span], arrived.at[1, step]),
            ]

        def down_copy(step):
            span = pl.ds(step * width, width)
            return pltpu.make_async_copy(
                down_ref.at[:, span], down_here.at[:, span], arrived.at[2, step]
            )

        for step in range(steps):
            for copy in copies(step):
                copy.start()
        for step in range(steps):
            down_copy(step).start()
        for place, ref in enumerate(ins):
            all_rows[place * count : (place + 1) * count] = ref[...]
        gate_sum = up_sum = None
        for step in range(steps):
            for copy in copies(step):
                copy.wait()
            span = slice(step * width, (step + 1) * width)
            piece = all_rows[:, span]
            gate_part = jnp.dot(piece, gate_here[span], preferred_element_type=jnp.float32)
            up_part = jnp.dot(piece, up_here[span], preferred_element_type=jnp.float32)
            gate_sum = gate_part if gate_sum is None else gate_sum + gate_part
            up_sum = up_part if up_sum is None else up_sum + up_part
        hidden = (jax.nn.silu(gate_sum) * up_sum).astype(jnp.bfloat16)
        for step in range(steps):
            down_copy(step).wait()
            span = slice(step * width, (step + 1) * width)
            answer = jnp.dot(
                hidden, down_here[:, span], preferred_element_type=jnp.float32
            ).astype(jnp.bfloat16)
            for place, ref in enumerate(outs):
                ref[:, span] = answer[place * count : (place + 1) * count]

    whole = pl.BlockSpec(memory_space=pltpu.VMEM)
    return pl.pallas_call(
        body,
        out_shape=[jax.ShapeDtypeStruct(block.shape, jnp.bfloat16) for block in blocks],
        in_specs=[whole] * number + [pl.BlockSpec(memory_space=pl.ANY)] * 3,
        out_specs=[whole] * number,
        scratch_shapes=[
            pltpu.VMEM(gate.shape, jnp.bfloat16),
            pltpu.VMEM(up.shape, jnp.bfloat16),
            pltpu.VMEM(down.shape, jnp.bfloat16),
            pltpu.VMEM((rows, model_width), jnp.bfloat16),
            pltpu.SemaphoreType.DMA((3, steps)),
        ],
        name="expert_rows",
    )(*blocks, gate, up, down)


def packed(wanted, choices, sibling_choices, tokens, sibling_tokens, blocks):
    cap = wanted.shape[0] // blocks

    def body(wanted_ref, choices_ref, sibling_ref, tokens_ref, other_ref, *outs):
        def rows_of(slots, tokens):
            taken = slots[0:1] == wanted_ref[...]
            for k in range(1, TOP):
                taken = taken | (slots[k : k + 1] == wanted_ref[...])
            table = jnp.where(taken, 1.0, 0.0).astype(jnp.bfloat16)
            return jnp.dot(table, tokens[...], preferred_element_type=jnp.float32)

        own = rows_of(choices_ref[...], tokens_ref)
        other = rows_of(sibling_ref[...], other_ref)
        for number, ref in enumerate(outs):
            span = slice(number * cap, (number + 1) * cap)
            ref[...] = jnp.concatenate([own[span], other[span]], axis=0).astype(jnp.bfloat16)

    whole = pl.BlockSpec(memory_space=pltpu.VMEM)
    return pl.pallas_call(
        body,
        out_shape=[jax.ShapeDtypeStruct((2 * cap, tokens.shape[1]), jnp.bfloat16)] * blocks,
        in_specs=[whole] * 5,
        out_specs=[whole] * blocks,
        name="packed",
    )(wanted, choices, sibling_choices, tokens, sibling_tokens)


def weighed(wanted, choices, own_blocks, sibling_blocks, added):
    blocks = len(own_blocks)
    cap = own_blocks[0].shape[0] // 2

    def body(wanted_ref, choices_ref, *refs):
        shares = None
        for k in range(TOP):
            share = jnp.where(
                choices_ref[:, k : k + 1] == wanted_ref[...],
                choices_ref[:, TOP + k : TOP + k + 1],
                0.0,
            )
            shares = share if shares is None else shares + share
        high = shares.astype(jnp.bfloat16)
        low = (shares - high.astype(jnp.float32)).astype(jnp.bfloat16)
        rows = jnp.concatenate(
            [ref[...][:cap] for ref in refs[:blocks]]
            + [ref[...][cap:] for ref in refs[blocks : 2 * blocks]],
            axis=0,
        )
        total = jnp.dot(high, rows, preferred_element_type=jnp.float32)
        total += jnp.dot(low, rows, preferred_element_type=jnp.float32)
        for ref in refs[2 * blocks : -1]:
            total += ref[...].astype(jnp.float32)
        refs[-1][...] = total.astype(jnp.bfloat16)

    whole = pl.BlockSpec(memory_space=pltpu.VMEM)
    return pl.pallas_call(
        body,
        out_shape=jax.ShapeDtypeStruct(
            (choices.shape[0], own_blocks[0].shape[1]), jnp.bfloat16
        ),
        in_specs=[whole] * (2 + 2 * blocks + len(added)),
        out_specs=whole,
        name="weighed",
    )(wanted, choices, *own_blocks, *sibling_blocks, *added)


def over_blocks(blocks):
    return [blocks[0]] + [swapped(block, 2 * k) for k, block in enumerate(blocks) if k]


def ring_step(value, steps=1):
    count = lax.axis_size("clip")
    ring = list(range(0, count, 2)) + sorted(range(1, count, 2), reverse=True)
    return lax.ppermute(
        value, "clip", [(ring[i], ring[(i + steps) % count]) for i in range(count)]
    )


def slots_and_gates(ids, gates, experts, capacity):
    positions = ids.shape[0]
    named = ids.T.reshape(1, TOP * positions)
    chosen = named == jnp.arange(experts, dtype=jnp.int32)[:, None]
    place = jnp.arange(TOP * positions, dtype=jnp.int32)
    before = (place[:, None] < place[None, :]).astype(jnp.bfloat16)
    earlier = jnp.dot(chosen.astype(jnp.bfloat16), before, preferred_element_type=jnp.float32)
    rank = jnp.sum(jnp.where(chosen, earlier, 0.0), axis=0)
    slots = named[0].astype(jnp.float32) * capacity + rank
    return jnp.concatenate([slots.reshape(TOP, positions), gates.T], axis=0)


def wanted_slots(capacity, odd):
    half = lax.axis_size("tm") // 2
    first = lax.axis_index("clip") * 2 * half
    slot = jnp.arange(half * capacity, dtype=jnp.int32)
    expert = first + (lax.axis_index("tm") ^ (2 * (slot // capacity) + odd))
    return (expert * capacity + slot % capacity).astype(jnp.float32)


def layer(
    tokens,
    spatial_queries,
    spatial_keys,
    spatial_values,
    spatial_proj,
    temporal_qkv,
    temporal_proj,
    frame_mask,
    expert_ids,
    gate_values,
    expert_gate,
    expert_up,
    expert_down,
):
    model_width = tokens.shape[3]
    positions = tokens.shape[2]
    tm_count = lax.axis_size("tm")
    clip_count = lax.axis_size("clip")
    experts = clip_count * tm_count
    per_block = positions // tm_count
    resident = tokens.reshape(positions, model_width)
    attended_space = spatial_mix(
        spatial_queries.reshape(positions, -1),
        spatial_keys.reshape(positions, -1),
        spatial_values.reshape(positions, -1),
    )
    third = temporal_qkv.shape[1] // 3
    parity = lax.axis_index("clip") % 2
    half = temporal_proj.shape[1] // 2
    mine, theirs = (
        lax.dynamic_slice_in_dim(temporal_qkv, which * third, third, axis=1)
        for which in (parity, 1 - parity)
    )
    value = temporal_qkv[:, 2 * third :]
    proj_mine, proj_theirs = (
        lax.dynamic_slice_in_dim(temporal_proj, which * half, half, axis=1)
        for which in (parity, 1 - parity)
    )
    spatial_direct = [direct_piece(spatial_proj, place) for place in range(2)]
    spatial_far = far_piece(after(spatial_direct[0], attended_space), 0)
    mine_direct = [direct_piece(after(mine, spatial_direct[0]), 0)]
    mine_direct += [direct_piece(after(mine, spatial_far), 1)]
    value_direct = [direct_piece(after(value, mine_direct[0]), 0)]
    value_direct += [direct_piece(after(value, mine_direct[1]), 1)]
    mine_far = far_piece(mine_direct[1], 1)
    value_far = far_piece(value_direct[0], 0)
    theirs_near = partner_pieces(mine_direct)
    theirs_far = partner_pieces([mine_far])[0]
    capacity = 2 * TOP * positions // experts
    choices = slots_and_gates(
        expert_ids.reshape(positions, TOP), gate_values.reshape(positions, TOP), experts, capacity
    )
    ring_choices = jnp.stack(
        [choices] + [ring_step(choices, step) for step in range(1, clip_count)]
    )
    sibling_choices = swapped(ring_choices, 1)
    turned_choices = jnp.swapaxes(ring_choices, 1, 2)
    even, odd = wanted_slots(capacity, 0), wanted_slots(capacity, 1)
    even_column, both_row = even[:, None], jnp.concatenate([even, odd])[None, :]
    first, normed = times_rows(
        attended_space, all_pieces(spatial_proj, spatial_direct, spatial_far), resident
    )
    allowed = frame_mask[0] == 1
    by_position = lax.all_to_all(
        normed.reshape(tm_count, per_block, model_width),
        "tm",
        split_axis=0,
        concat_axis=0,
        tiled=True,
    )
    frames = by_position.shape[0]
    by_position = after(
        by_position.reshape(frames * per_block, model_width),
        ring_choices,
        sibling_choices,
        turned_choices,
        even_column,
        both_row,
    )
    proj_direct = [
        direct_piece(after(proj_mine, value_direct[place], by_position), place)
        for place in range(2)
    ]

    def projected(*pieces):
        return times_rows(by_position, all_pieces(*pieces, earlier=(by_position,)))

    first_pair = [projected(mine, mine_direct, mine_far), projected(theirs, theirs_near, theirs_far)]
    proj_far = far_piece(after(proj_direct[0], *first_pair), 0)
    proj_near = partner_pieces([after(p, *first_pair) for p in proj_direct])
    values = projected(value, value_direct, value_far)
    proj_partner = partner_pieces([after(proj_far, values)])[0]
    even_plane = parity == 0
    queries = jnp.where(even_plane, first_pair[0], first_pair[1])
    keys = jnp.where(even_plane, first_pair[1], first_pair[0])
    attended_time = temporal_mix(
        *(part.reshape(frames, per_block, third) for part in (queries, keys, values)), allowed
    ).reshape(frames * per_block, third)
    sides = [
        times_rows(attended_time, all_pieces(*pieces, earlier=(values,)))
        for pieces in (
            (proj_mine, proj_direct, proj_far),
            (proj_theirs, proj_near, proj_partner),
        )
    ]
    update_rows = jnp.concatenate(
        [jnp.where(even_plane, sides[0], sides[1]), jnp.where(even_plane, sides[1], sides[0])],
        axis=1,
    )
    returned = lax.all_to_all(
        update_rows.reshape(frames, per_block, model_width),
        "tm",
        split_axis=0,
        concat_axis=0,
        tiled=True,
    )
    temporal_update = returned.reshape(positions, model_width)
    second = (first.astype(jnp.float32) + temporal_update.astype(jnp.float32)).astype(jnp.bfloat16)
    routed = rms_normed(second)
    blocks = tm_count // 2
    experts_here = (expert_gate[0], expert_up[0], expert_down[0])
    received, answers, returned_rows = [], [], []

    def answer(arrived):
        given = expert_rows(arrived, *experts_here)
        answers.append(given[0])
        own = over_blocks(given)
        returned_rows.append((own, [swapped(block, 1) for block in own]))

    def late(arrived, *earlier):
        return [after(arrived[0], *earlier)] + arrived[1:]

    tokens_here = routed
    for step in range(clip_count):
        if step:
            tokens_here = ring_step(tokens_here)
        tokens_now = after(tokens_here, answers[step - 2]) if step > 1 else tokens_here
        sibling_tokens = swapped(tokens_now, 1)
        outgoing = packed(
            even_column,
            ring_choices[step],
            sibling_choices[step],
            tokens_now,
            sibling_tokens,
            blocks,
        )
        received.append(over_blocks(outgoing))
        if step:
            answer(late(received[step - 1], *outgoing))
    carried, carried_here = [], []
    for step in range(1, clip_count):
        if len(returned_rows) == step or step == 2:
            answer(late(received[-1], *carried_here))
        own, other = returned_rows[step]
        carried_here = [weighed(both_row, turned_choices[step], own, other, carried)]
        carried = [ring_step(carried_here[0])]
    layer_out = weighed(both_row, turned_choices[0], *returned_rows[0], [second] + carried)
    return layer_out.reshape(tokens.shape)


def solution(mesh):
    placed = (
        P("clip", "tm", None, None),
        P("clip", "tm", None, None),
        P("clip", "tm", None, None),
        P("clip", "tm", None, None),
        P("tm", None),
        P("tm", None),
        P("tm", None),
        P("clip", None, None),
        P("clip", "tm", None, None),
        P("clip", "tm", None, None),
        P(("clip", "tm"), None, None),
        P(("clip", "tm"), None, None),
        P(("clip", "tm"), None, None),
    )
    return jax.shard_map(
        layer, mesh=mesh, in_specs=placed, out_specs=P("clip", "tm", None, None), check_vma=False
    )
```

time: 432 us -> 413 us (0.956)
  blocking collectives: 194 us -> 19.1 us
  Pallas kernels: 0 us -> 99.1 us
  starting transfers between devices: 7.38 us -> 84 us
  matrix products: 57 us -> 8.16 us
  waiting for transfers between devices: 149 us -> 169 us
  local copies, waits for them, and re-layouts: 5.99 us -> 23.1 us
  between operations: 13.3 us -> 1.09 us
    all_to_all x2 -> x1, blocking collectives: 194 us -> 19.1 us  [layer(): lax.all_to_all(update_rows.reshape(frames, per_block, model_width), 'tm',...]
    ppermute x0 -> x96, waiting for transfers between devices: none -> 169 us  [the longest x81 104 us: swapped(): return lax.ppermute(piece, 'tm', [(i, i ^ bit) for i in range(count)])]
    all_gather x3 -> x0, waiting for transfers between devices: 108 us -> none  [the longest x1 49.2 us: temporal_inputs(): lax.all_gather(qkv_rows, 'tm', axis=0, tiled=True)]
    pallas_call x0 -> x18, Pallas kernels: none -> 99.1 us  [the longest x4 44.2 us: expert_rows(): pl.pallas_call(body, out_shape=[jax.ShapeDtypeStruct(block.shape, jnp.bfl...]
    ppermute x0 -> x96, starting transfers between devices: none -> 80.3 us  [the longest x81 55 us: swapped(): return lax.ppermute(piece, 'tm', [(i, i ^ bit) for i in range(count)])]
    dot_general x7 -> x1, matrix products: 48.9 us -> 0.2 us  [slots_and_gates(): jnp.dot(chosen.astype(jnp.bfloat16), before, preferred_element_type=jnp.f...]
    all_to_all x2 -> x1, waiting for transfers between devices: 38.1 us -> 0.01 us  [layer(): lax.all_to_all(normed.reshape(tm_count, per_block, model_width), 'tm', sp...]
    unnamed x22 -> x169, local copies, waits for them, and re-layouts: 4.73 us -> 16.9 us
  transfers between devices with their start and end apart: 5 -> 97, of which waited for: 5 -> 43; matrix products, arithmetic and copies ran while one was open for 6% -> 5% of each run, Pallas kernels for 0% -> 20%
where the time goes in v1:
time: 413 us; the launch traced here: 408 us
  waiting for transfers between devices  169 us (41%)
  Pallas kernels  99.1 us (24%)
  starting transfers between devices  84 us (20%)
  local copies, waits for them, and re-layouts  23.1 us (6%)
  blocking collectives  19.1 us (5%)
  matrix products  8.16 us (2%)
  other arithmetic  4.36 us (1%)
    ppermute x81, waiting for transfers between devices, swapped(): return lax.ppermute(piece, 'tm', [(i, i ^ bit) for i in range(count)])  104 us
    ppermute x81, starting transfers between devices, swapped(): return lax.ppermute(piece, 'tm', [(i, i ^ bit) for i in range(count)])  55 us
    pallas_call x4, Pallas kernels, expert_rows(): pl.pallas_call(body, out_shape=[jax.ShapeDtypeStruct(block.shape, jnp.bfl...  44.2 us
    ppermute x9, waiting for transfers between devices, ring_step(): lax.ppermute(value, 'clip', [(ring[i], ring[(i + steps) % count]) for i i...  41.5 us
    pallas_call x6, Pallas kernels, times_rows(): pl.pallas_call(body, out_shape=[out, out] if extra else out, in_specs=[pl...  27.3 us
    ppermute x6, waiting for transfers between devices, partner_pieces(): lax.ppermute(piece, 'clip', [(i, i ^ 1) for i in range(count)])  23.9 us
    all_to_all x1, blocking collectives, layer(): lax.all_to_all(update_rows.reshape(frames, per_block, model_width), 'tm',...  19.1 us
    ppermute x9, starting transfers between devices, ring_step(): lax.ppermute(value, 'clip', [(ring[i], ring[(i + steps) % count]) for i i...  17.1 us
  transfers between devices with their start and end apart: 97, of which 43 were waited for; matrix products, arithmetic and copies ran while one was open for 5% of the time, Pallas kernels for 20%

profile of v1, /device:TPU:0, one launch (start us, length us, event | category | flops | bytes accessed | tf_op | source)
XLA Modules:
  0.0 408.0 jit_solution(9458081889330588979)
XLA Ops:
  20.5 7.8 %collective-permute-done.6.refs_3_ = bf16[128,2048]{1,0:T(8,128)(2,1)} collective-permute-done((bf16[128,2048]{1,0:T(8,128)(2,1)S(1)}, bf16[128,2048]{1,0:T(8,128)(2,1)}, u32[]{:S(2)}, u32[]{:S(2)}) %collective-permute-start.6) | collective-permute-done | bytes 524320 | tf_op jit(solution)/shard_map/ppermute | solution.py:72
  33.8 6.3 %times_rows.6 = (bf16[256,2048]{1,0:T(8,128)(2,1)}, bf16[256,2048]{1,0:T(8,128)(2,1)}) custom-call(s32[8]{0:T(128)} %stack.41.places_ref, bf16[256,1024]{1,0:T(8,128)(2,1)} %copy.73.left_ref, bf16[128,2048]{1,0:T(8,128)(2,1)} %refs_0_.1, bf16[128,2048]{1,0:T(8,128)(2,1)} %copy-done.20, bf16[128,2048]{1,0:T(8,128)(2,1)} %copy-done.21, ...), custom_call_target="tpu_custom_call" | custom-call | tf_op jit(solution)/shard_map/times_rows/pallas_call | solution.py:142
  49.6 8.2 %collective-permute-done.2.choices_ref = f32[4,256]{1,0:T(4,128)S(1)} collective-permute-done((f32[4,256]{1,0:T(4,128)S(1)}, f32[4,256]{1,0:T(4,128)S(1)}, u32[]{:S(2)}, u32[]{:S(2)}) %collective-permute-start.2) | collective-permute-done | bytes 4128 | tf_op jit(solution)/shard_map/ppermute | solution.py:295
  75.2 8.2 %collective-permute-done.26.refs_2_ = bf16[256,1024]{1,0:T(8,128)(2,1)} collective-permute-done((bf16[256,1024]{1,0:T(8,128)(2,1)}, bf16[256,1024]{1,0:T(8,128)(2,1)}, u32[]{:S(2)}, u32[]{:S(2)}) %collective-permute-start.26) | collective-permute-done | bytes 524320 | tf_op jit(solution)/shard_map/ppermute | solution.py:91
  86.6 7.3 %collective-permute-done.27.refs_3_ = bf16[256,1024]{1,0:T(8,128)(2,1)} collective-permute-done((bf16[256,1024]{1,0:T(8,128)(2,1)}, bf16[256,1024]{1,0:T(8,128)(2,1)}, u32[]{:S(2)}, u32[]{:S(2)}) %collective-permute-start.27) | collective-permute-done | bytes 524320 | tf_op jit(solution)/shard_map/ppermute | solution.py:91
  99.4 4.6 %times_rows.7 = bf16[256,1024]{1,0:T(8,128)(2,1)} custom-call(s32[8]{0:T(128)} %stack.41.places_ref, bf16[256,2048]{1,0:T(8,128)(2,1)} %bitcast.101, bf16[256,1024]{1,0:T(8,128)(2,1)} %copy-done.6, bf16[256,1024]{1,0:T(8,128)(2,1)} %collective-permute-done.12.refs_1_, bf16[256,1024]{1,0:T(8,128)(2,1)} %collective-permute-done.14.refs_2_, ...), custom_call_target="tpu_custom_call" | custom-call | tf_op jit(solution)/shard_map/times_rows/pallas_call | solution.py:142
  105.6 4.5 %times_rows.8 = bf16[256,1024]{1,0:T(8,128)(2,1)} custom-call(s32[8]{0:T(128)} %stack.41.places_ref, bf16[256,2048]{1,0:T(8,128)(2,1)} %bitcast.102, bf16[256,1024]{1,0:T(8,128)(2,1)} %copy-done.5, bf16[256,1024]{1,0:T(8,128)(2,1)} %collective-permute-done.11.refs_1_, bf16[256,1024]{1,0:T(8,128)(2,1)} %collective-permute-done.13.refs_2_, ...), custom_call_target="tpu_custom_call" | custom-call | tf_op jit(solution)/shard_map/times_rows/pallas_call | solution.py:142
  110.7 4.5 %times_rows.9 = bf16[256,1024]{1,0:T(8,128)(2,1)} custom-call(s32[8]{0:T(128)} %stack.41.places_ref, bf16[256,2048]{1,0:T(8,128)(2,1)} %bitcast.103, bf16[256,1024]{1,0:T(8,128)(2,1)} %copy-done.4, bf16[256,1024]{1,0:T(8,128)(2,1)} %collective-permute-done.25.refs_1_, bf16[256,1024]{1,0:T(8,128)(2,1)} %collective-permute-done.26.refs_2_, ...), custom_call_target="tpu_custom_call" | custom-call | tf_op jit(solution)/shard_map/times_rows/pallas_call | solution.py:142
  119.8 4.1 %collective-permute-done.34.refs_3_ = bf16[128,1024]{1,0:T(8,128)(2,1)} collective-permute-done((bf16[128,1024]{1,0:T(8,128)(2,1)}, bf16[128,1024]{1,0:T(8,128)(2,1)}, u32[]{:S(2)}, u32[]{:S(2)}) %collective-permute-start.34) | collective-permute-done | bytes 262176 | tf_op jit(solution)/shard_map/ppermute | solution.py:72
  128.9 4.4 %collective-permute-done.40.refs_2_ = bf16[128,1024]{1,0:T(8,128)(2,1)} collective-permute-done((bf16[128,1024]{1,0:T(8,128)(2,1)}, bf16[128,1024]{1,0:T(8,128)(2,1)}, u32[]{:S(2)}, u32[]{:S(2)}) %collective-permute-start.40) | collective-permute-done | bytes 262176 | tf_op jit(solution)/shard_map/ppermute | solution.py:91
  151.3 19.1 %all_to_all.10 = bf16[8,32,2048]{2,1,0:T(8,128)(2,1)S(1)} all-to-all(bf16[8,32,2048]{2,1,0:T(8,128)(2,1)S(1)} %bitcast.106), channel_id=1, replica_groups=mesh['clip'=4,'tm'=8] {'tm'}, dimensions={0} | all-to-all | bytes 2097152 | tf_op jit(solution)/shard_map/all_to_all | solution.py:430
  173.9 21.9 %collective-permute-done.47.tokens_ref = bf16[256,2048]{1,0:T(8,128)(2,1)} collective-permute-done((bf16[256,2048]{1,0:T(8,128)(2,1)S(1)}, bf16[256,2048]{1,0:T(8,128)(2,1)}, u32[]{:S(2)}, u32[]{:S(2)}) %collective-permute-start.47) | collective-permute-done | bytes 1048608 | tf_op jit(solution)/shard_map/ppermute | solution.py:295
  195.8 4.0 collective-permute-start.59
  213.8 5.8 %collective-permute-done.50.refs_2_ = bf16[64,2048]{1,0:T(8,128)(2,1)S(1)} collective-permute-done((bf16[64,2048]{1,0:T(8,128)(2,1)}, bf16[64,2048]{1,0:T(8,128)(2,1)S(1)}, u32[]{:S(2)}, u32[]{:S(2)}) %collective-permute-start.50) | collective-permute-done | bytes 262176 | tf_op jit(solution)/shard_map/ppermute | solution.py:72
  220.3 11.0 %expert_rows.4 = (bf16[64,2048]{1,0:T(8,128)(2,1)}, bf16[64,2048]{1,0:T(8,128)(2,1)}, bf16[64,2048]{1,0:T(8,128)(2,1)}, bf16[64,2048]{1,0:T(8,128)(2,1)}) custom-call(bf16[64,2048]{1,0:T(8,128)(2,1)} %get-tuple-element.112.refs_0_, bf16[64,2048]{1,0:T(8,128)(2,1)} %copy-done.28, bf16[64,2048]{1,0:T(8,128)(2,1)} %copy-done.30, bf16[64,2048]{1,0:T(8,128)(2,1)} %copy-done.32, ...), custom_call_target="tpu_custom_call" | custom-call | tf_op jit(solution)/shard_map/expert_rows/pallas_call | solution.py:207
  241.4 5.4 %collective-permute-done.63.refs_2_ = bf16[64,2048]{1,0:T(8,128)(2,1)S(1)} collective-permute-done((bf16[64,2048]{1,0:T(8,128)(2,1)}, bf16[64,2048]{1,0:T(8,128)(2,1)S(1)}, u32[]{:S(2)}, u32[]{:S(2)}) %collective-permute-start.63) | collective-permute-done | bytes 262176 | tf_op jit(solution)/shard_map/ppermute | solution.py:72
  248.2 11.0 %expert_rows.5 = (bf16[64,2048]{1,0:T(8,128)(2,1)}, bf16[64,2048]{1,0:T(8,128)(2,1)}, bf16[64,2048]{1,0:T(8,128)(2,1)}, bf16[64,2048]{1,0:T(8,128)(2,1)}) custom-call(bf16[64,2048]{1,0:T(8,128)(2,1)} %get-tuple-element.125.refs_0_, bf16[64,2048]{1,0:T(8,128)(2,1)} %copy-done.29, bf16[64,2048]{1,0:T(8,128)(2,1)} %copy-done.31, bf16[64,2048]{1,0:T(8,128)(2,1)} %copy-done.33, ...), custom_call_target="tpu_custom_call" | custom-call | tf_op jit(solution)/shard_map/expert_rows/pallas_call | solution.py:207
  262.9 5.9 %collective-permute-done.66.refs_1_ = bf16[64,2048]{1,0:T(8,128)(2,1)S(1)} collective-permute-done((bf16[64,2048]{1,0:T(8,128)(2,1)}, bf16[64,2048]{1,0:T(8,128)(2,1)S(1)}, u32[]{:S(2)}, u32[]{:S(2)}) %collective-permute-start.66) | collective-permute-done | bytes 262176 | tf_op jit(solution)/shard_map/ppermute | solution.py:72
  268.8 6.0 %collective-permute-done.67.refs_2_ = bf16[64,2048]{1,0:T(8,128)(2,1)S(1)} collective-permute-done((bf16[64,2048]{1,0:T(8,128)(2,1)}, bf16[64,2048]{1,0:T(8,128)(2,1)S(1)}, u32[]{:S(2)}, u32[]{:S(2)}) %collective-permute-start.67) | collective-permute-done | bytes 262176 | tf_op jit(solution)/shard_map/ppermute | solution.py:72
  292.4 5.1 %collective-permute-done.84.refs_2_ = bf16[64,2048]{1,0:T(8,128)(2,1)} collective-permute-done((bf16[64,2048]{1,0:T(8,128)(2,1)}, bf16[64,2048]{1,0:T(8,128)(2,1)}, u32[]{:S(2)}, u32[]{:S(2)}) %collective-permute-start.84) | collective-permute-done | bytes 262176 | tf_op jit(solution)/shard_map/ppermute | solution.py:72
  297.6 11.0 %expert_rows.7 = (bf16[64,2048]{1,0:T(8,128)(2,1)}, bf16[64,2048]{1,0:T(8,128)(2,1)}, bf16[64,2048]{1,0:T(8,128)(2,1)}, bf16[64,2048]{1,0:T(8,128)(2,1)}) custom-call(bf16[64,2048]{1,0:T(8,128)(2,1)} %get-tuple-element.140.refs_0_, bf16[64,2048]{1,0:T(8,128)(2,1)} %copy-done.27, bf16[64,2048]{1,0:T(8,128)(2,1)} %collective-permute-done.84.refs_2_, ...), custom_call_target="tpu_custom_call" | custom-call | tf_op jit(solution)/shard_map/expert_rows/pallas_call | solution.py:207
  312.2 5.9 %collective-permute-done.86.refs_1_ = bf16[64,2048]{1,0:T(8,128)(2,1)S(1)} collective-permute-done((bf16[64,2048]{1,0:T(8,128)(2,1)}, bf16[64,2048]{1,0:T(8,128)(2,1)S(1)}, u32[]{:S(2)}, u32[]{:S(2)}) %collective-permute-start.86) | collective-permute-done | bytes 262176 | tf_op jit(solution)/shard_map/ppermute | solution.py:72
  318.1 4.2 %collective-permute-done.87.refs_2_ = bf16[64,2048]{1,0:T(8,128)(2,1)S(1)} collective-permute-done((bf16[64,2048]{1,0:T(8,128)(2,1)}, bf16[64,2048]{1,0:T(8,128)(2,1)S(1)}, u32[]{:S(2)}, u32[]{:S(2)}) %collective-permute-start.87) | collective-permute-done | bytes 262176 | tf_op jit(solution)/shard_map/ppermute | solution.py:72
  333.3 5.9 %collective-permute-done.73.refs_1_ = bf16[64,2048]{1,0:T(8,128)(2,1)S(1)} collective-permute-done((bf16[64,2048]{1,0:T(8,128)(2,1)}, bf16[64,2048]{1,0:T(8,128)(2,1)S(1)}, u32[]{:S(2)}, u32[]{:S(2)}) %collective-permute-start.73) | collective-permute-done | bytes 262176 | tf_op jit(solution)/shard_map/ppermute | solution.py:72
  339.2 4.9 %collective-permute-done.74.refs_2_ = bf16[64,2048]{1,0:T(8,128)(2,1)S(1)} collective-permute-done((bf16[64,2048]{1,0:T(8,128)(2,1)S(1)}, bf16[64,2048]{1,0:T(8,128)(2,1)S(1)}, u32[]{:S(2)}, u32[]{:S(2)}) %collective-permute-start.74) | collective-permute-done | bytes 262176 | tf_op jit(solution)/shard_map/ppermute | solution.py:72
  345.4 11.1 %expert_rows.6 = (bf16[64,2048]{1,0:T(8,128)(2,1)}, bf16[64,2048]{1,0:T(8,128)(2,1)}, bf16[64,2048]{1,0:T(8,128)(2,1)}, bf16[64,2048]{1,0:T(8,128)(2,1)}) custom-call(bf16[64,2048]{1,0:T(8,128)(2,1)} %get-tuple-element.132.refs_0_, bf16[64,2048]{1,0:T(8,128)(2,1)} %copy-done.34, bf16[64,2048]{1,0:T(8,128)(2,1)} %copy-done.35, bf16[64,2048]{1,0:T(8,128)(2,1)} %copy-done.36, ...), custom_call_target="tpu_custom_call" | custom-call | tf_op jit(solution)/shard_map/expert_rows/pallas_call | solution.py:207
  360.1 5.9 %collective-permute-done.76.refs_1_ = bf16[64,2048]{1,0:T(8,128)(2,1)S(1)} collective-permute-done((bf16[64,2048]{1,0:T(8,128)(2,1)}, bf16[64,2048]{1,0:T(8,128)(2,1)S(1)}, u32[]{:S(2)}, u32[]{:S(2)}) %collective-permute-start.76) | collective-permute-done | bytes 262176 | tf_op jit(solution)/shard_map/ppermute | solution.py:72
  366.0 4.0 collective-permute-done.77.refs_2_
  383.0 5.9 %collective-permute-done.52.refs_1_ = bf16[64,2048]{1,0:T(8,128)(2,1)S(1)} collective-permute-done((bf16[64,2048]{1,0:T(8,128)(2,1)}, bf16[64,2048]{1,0:T(8,128)(2,1)S(1)}, u32[]{:S(2)}, u32[]{:S(2)}) %collective-permute-start.52) | collective-permute-done | bytes 262176 | tf_op jit(solution)/shard_map/ppermute | solution.py:72
  388.9 5.1 %collective-permute-done.53.refs_2_ = bf16[64,2048]{1,0:T(8,128)(2,1)S(1)} collective-permute-done((bf16[64,2048]{1,0:T(8,128)(2,1)}, bf16[64,2048]{1,0:T(8,128)(2,1)S(1)}, u32[]{:S(2)}, u32[]{:S(2)}) %collective-permute-start.53) | collective-permute-done | bytes 262176 | tf_op jit(solution)/shard_map/ppermute | solution.py:72
  395.9 6.6 %collective-permute-done.95.refs_9_ = bf16[256,2048]{1,0:T(8,128)(2,1)S(1)} collective-permute-done((bf16[256,2048]{1,0:T(8,128)(2,1)}, bf16[256,2048]{1,0:T(8,128)(2,1)S(1)}, u32[]{:S(2)}, u32[]{:S(2)}) %collective-permute-start.95) | collective-permute-done | bytes 1048608 | tf_op jit(solution)/shard_map/ppermute | solution.py:295
  403.5 4.2 %weighed.7 = bf16[256,2048]{1,0:T(8,128)(2,1)} custom-call(f32[1,256]{1,0:T(1,128)} %bitcast.124, f32[256,4]{1,0:T(8,128)} %get-tuple-element.157.choices_ref, bf16[64,2048]{1,0:T(8,128)(2,1)} %get-tuple-element.116.refs_0_, bf16[64,2048]{1,0:T(8,128)(2,1)} %copy-done.38, bf16[64,2048]{1,0:T(8,128)(2,1)} %copy-done.42, bf16[64,2048]{1,0:T(8,128)(2,1)} %copy-done.46, ...), custom_call_target="tpu_custom_call" | custom-call | tf_op jit(solution)/shard_map/weighed/pallas_call | solution.py:277
  (379 shorter events, 177.0 us)
Async XLA Ops:
  0.0 15.1 %collective-permute-start.4 = (bf16[128,2048]{1,0:T(8,128)(2,1)}, bf16[128,2048]{1,0:T(8,128)(2,1)S(1)}, u32[]{:S(2)}, u32[]{:S(2)}) collective-permute-start(bf16[128,2048]{1,0:T(8,128)(2,1)} %refs_0_.1), channel_id=1, source_target_pairs={{0,4},{1,5},{2,6},{3,7},{4,0},{5,1},{6,2},{7,3},{8,12},{9,13},{10,... | collective-permute-start | bytes 1572872 | tf_op jit(solution)/shard_map/ppermute | solution.py:72
  3.0 17.5 %collective-permute-start.5 = (bf16[128,2048]{1,0:T(8,128)(2,1)}, bf16[128,2048]{1,0:T(8,128)(2,1)S(1)}, u32[]{:S(2)}, u32[]{:S(2)}) collective-permute-start(bf16[128,2048]{1,0:T(8,128)(2,1)} %refs_0_.1), channel_id=1, source_target_pairs={{0,2},{1,3},{2,0},{3,1},{4,6},{5,7},{6,4},{7,5},{8,10},{9,11},{10,... | collective-permute-start | bytes 1572872 | tf_op jit(solution)/shard_map/ppermute | solution.py:72
  20.0 13.8 %collective-permute-start.8 = (bf16[128,2048]{1,0:T(8,128)(2,1)S(1)}, bf16[128,2048]{1,0:T(8,128)(2,1)}, u32[]{:S(2)}, u32[]{:S(2)}) collective-permute-start(bf16[128,2048]{1,0:T(8,128)(2,1)S(1)} %collective-permute-done.4.refs_1_), channel_id=1, source_target_pairs={{0,1},{1,0},{2,3},{3,2},{4,5},{5,4},{6,7},{7,6},{8,9},{9,8},{10,11... | collective-permute-start | bytes 1572872 | tf_op jit(solution)/shard_map/ppermute | solution.py:72
  31.1 14.6 %collective-permute-start.13 = (bf16[256,1024]{1,0:T(8,128)(2,1)S(1)}, bf16[256,1024]{1,0:T(8,128)(2,1)}, u32[]{:S(2)}, u32[]{:S(2)}) collective-permute-start(bf16[256,1024]{1,0:T(8,128)(2,1)S(1)} %get-tuple-element.87.refs_0_), channel_id=1, source_target_pairs={{0,2},{1,3},{2,0},{3,1},{4,6},{5,7},{6,4},{7,5},{8,10},{9,11},{10,... | collective-permute-start | bytes 1572872 | tf_op jit(solution)/shard_map/ppermute | solution.py:72
  32.3 37.6 %collective-permute-start.12 = (bf16[256,1024]{1,0:T(8,128)(2,1)S(1)}, bf16[256,1024]{1,0:T(8,128)(2,1)}, u32[]{:S(2)}, u32[]{:S(2)}) collective-permute-start(bf16[256,1024]{1,0:T(8,128)(2,1)S(1)} %get-tuple-element.83.refs_0_), channel_id=1, source_target_pairs={{0,4},{1,5},{2,6},{3,7},{4,0},{5,1},{6,2},{7,3},{8,12},{9,13},{10,... | collective-permute-start | bytes 1572872 | tf_op jit(solution)/shard_map/ppermute | solution.py:72
  40.1 33.5 %all-to-all-start = ((bf16[8,32,2048]{2,1,0:T(8,128)(2,1)}), bf16[8,32,2048]{2,1,0:T(8,128)(2,1)S(1)}, u32[]{:S(2)}, u32[]{:S(2)}) async-start(bf16[8,32,2048]{2,1,0:T(8,128)(2,1)} %bitcast.110), calls=%async_computation | async-start | bytes 2097152 | tf_op jit(solution)/shard_map/all_to_all | solution.py:384
  44.0 29.5 %collective-permute-start.25 = (bf16[256,1024]{1,0:T(8,128)(2,1)}, bf16[256,1024]{1,0:T(8,128)(2,1)}, u32[]{:S(2)}, u32[]{:S(2)}) collective-permute-start(bf16[256,1024]{1,0:T(8,128)(2,1)} %collective-permute-done.11.refs_1_), channel_id=1, source_target_pairs={{0,8},{8,0},{16,24},{24,16},{1,9},{9,1},{17,25},{25,17},{2,10},{10... | collective-permute-start | bytes 1572872 | tf_op jit(solution)/shard_map/ppermute | solution.py:91
  45.7 28.0 %collective-permute-start.14 = (bf16[256,1024]{1,0:T(8,128)(2,1)S(1)}, bf16[256,1024]{1,0:T(8,128)(2,1)}, u32[]{:S(2)}, u32[]{:S(2)}) collective-permute-start(bf16[256,1024]{1,0:T(8,128)(2,1)S(1)} %get-tuple-element.83.refs_0_), channel_id=1, source_target_pairs={{0,2},{1,3},{2,0},{3,1},{4,6},{5,7},{6,4},{7,5},{8,10},{9,11},{10,... | collective-permute-start | bytes 1572872 | tf_op jit(solution)/shard_map/ppermute | solution.py:72
  47.6 25.4 %collective-permute-start.20 = (bf16[256,1024]{1,0:T(8,128)(2,1)}, bf16[256,1024]{1,0:T(8,128)(2,1)}, u32[]{:S(2)}, u32[]{:S(2)}) collective-permute-start(bf16[256,1024]{1,0:T(8,128)(2,1)} %collective-permute-done.13.refs_2_), channel_id=1, source_target_pairs={{0,4},{1,5},{2,6},{3,7},{4,0},{5,1},{6,2},{7,3},{8,12},{9,13},{10,... | collective-permute-start | bytes 1572872 | tf_op jit(solution)/shard_map/ppermute | solution.py:72
  68.3 15.1 %collective-permute-start.26 = (bf16[256,1024]{1,0:T(8,128)(2,1)}, bf16[256,1024]{1,0:T(8,128)(2,1)}, u32[]{:S(2)}, u32[]{:S(2)}) collective-permute-start(bf16[256,1024]{1,0:T(8,128)(2,1)} %collective-permute-done.13.refs_2_), channel_id=1, source_target_pairs={{0,8},{8,0},{16,24},{24,16},{1,9},{9,1},{17,25},{25,17},{2,10},{10... | collective-permute-start | bytes 1572872 | tf_op jit(solution)/shard_map/ppermute | solution.py:91
  69.9 15.2 %collective-permute-start.15 = (bf16[256,1024]{1,0:T(8,128)(2,1)}, bf16[256,1024]{1,0:T(8,128)(2,1)}, u32[]{:S(2)}, u32[]{:S(2)}) collective-permute-start(bf16[256,1024]{1,0:T(8,128)(2,1)} %collective-permute-done.12.refs_1_), channel_id=1, source_target_pairs={{0,2},{1,3},{2,0},{3,1},{4,6},{5,7},{6,4},{7,5},{8,10},{9,11},{10,... | collective-permute-start | bytes 1572872 | tf_op jit(solution)/shard_map/ppermute | solution.py:72
  73.0 20.8 %collective-permute-start.27 = (bf16[256,1024]{1,0:T(8,128)(2,1)}, bf16[256,1024]{1,0:T(8,128)(2,1)}, u32[]{:S(2)}, u32[]{:S(2)}) collective-permute-start(bf16[256,1024]{1,0:T(8,128)(2,1)} %collective-permute-done.20.refs_3_), channel_id=1, source_target_pairs={{0,8},{8,0},{16,24},{24,16},{1,9},{9,1},{17,25},{25,17},{2,10},{10... | collective-permute-start | bytes 1572872 | tf_op jit(solution)/shard_map/ppermute | solution.py:91
  73.6 20.9 %collective-permute-start.21 = (bf16[256,1024]{1,0:T(8,128)(2,1)S(1)}, bf16[256,1024]{1,0:T(8,128)(2,1)}, u32[]{:S(2)}, u32[]{:S(2)}) collective-permute-start(bf16[256,1024]{1,0:T(8,128)(2,1)S(1)} %get-tuple-element.87.refs_0_), channel_id=1, source_target_pairs={{0,1},{1,0},{2,3},{3,2},{4,5},{5,4},{6,7},{7,6},{8,9},{9,8},{10,11... | collective-permute-start | bytes 1572872 | tf_op jit(solution)/shard_map/ppermute | solution.py:72
  73.7 21.2 %collective-permute-start.22 = (bf16[256,1024]{1,0:T(8,128)(2,1)}, bf16[256,1024]{1,0:T(8,128)(2,1)}, u32[]{:S(2)}, u32[]{:S(2)}) collective-permute-start(bf16[256,1024]{1,0:T(8,128)(2,1)} %collective-permute-done.11.refs_1_), channel_id=1, source_target_pairs={{0,1},{1,0},{2,3},{3,2},{4,5},{5,4},{6,7},{7,6},{8,9},{9,8},{10,11... | collective-permute-start | bytes 1572872 | tf_op jit(solution)/shard_map/ppermute | solution.py:72
  105.1 32.2 %collective-permute-start.35 = (bf16[128,1024]{1,0:T(8,128)(2,1)S(1)}, bf16[128,1024]{1,0:T(8,128)(2,1)S(1)}, u32[]{:S(2)}, u32[]{:S(2)}) collective-permute-start(bf16[128,1024]{1,0:T(8,128)(2,1)S(1)} %copy-done.18), channel_id=1, source_target_pairs={{0,1},{1,0},{2,3},{3,2},{4,5},{5,4},{6,7},{7,6},{8,9},{9,8},{10,11... | collective-permute-start | bytes 786440 | tf_op jit(solution)/shard_map/ppermute | solution.py:72
  110.1 27.7 %collective-permute-start.36 = (bf16[128,1024]{1,0:T(8,128)(2,1)}, bf16[128,1024]{1,0:T(8,128)(2,1)}, u32[]{:S(2)}, u32[]{:S(2)}) collective-permute-start(bf16[128,1024]{1,0:T(8,128)(2,1)} %collective-permute-done.32.refs_1_), channel_id=1, source_target_pairs={{0,1},{1,0},{2,3},{3,2},{4,5},{5,4},{6,7},{7,6},{8,9},{9,8},{10,11... | collective-permute-start | bytes 786440 | tf_op jit(solution)/shard_map/ppermute | solution.py:72
  110.3 27.6 %collective-permute-start.37 = (bf16[128,1024]{1,0:T(8,128)(2,1)}, bf16[128,1024]{1,0:T(8,128)(2,1)}, u32[]{:S(2)}, u32[]{:S(2)}) collective-permute-start(bf16[128,1024]{1,0:T(8,128)(2,1)} %collective-permute-done.33.refs_2_), channel_id=1, source_target_pairs={{0,1},{1,0},{2,3},{3,2},{4,5},{5,4},{6,7},{7,6},{8,9},{9,8},{10,11... | collective-permute-start | bytes 786440 | tf_op jit(solution)/shard_map/ppermute | solution.py:72
  171.2 24.5 %collective-permute-start.47 = (bf16[256,2048]{1,0:T(8,128)(2,1)S(1)}, bf16[256,2048]{1,0:T(8,128)(2,1)}, u32[]{:S(2)}, u32[]{:S(2)}) collective-permute-start(bf16[256,2048]{1,0:T(8,128)(2,1)S(1)} %fusion.3.tokens_ref), channel_id=1, source_target_pairs={{0,16},{16,24},{24,8},{8,0},{1,17},{17,25},{25,9},{9,1},{2,18},{18... | collective-permute-start | bytes 3145736 | tf_op jit(solution)/shard_map/ppermute | solution.py:295
  173.9 26.5 %collective-permute-start.46 = (bf16[256,2048]{1,0:T(8,128)(2,1)S(1)}, bf16[256,2048]{1,0:T(8,128)(2,1)S(1)}, u32[]{:S(2)}, u32[]{:S(2)}) collective-permute-start(bf16[256,2048]{1,0:T(8,128)(2,1)S(1)} %fusion.3.tokens_ref), channel_id=1, source_target_pairs={{0,1},{1,0},{2,3},{3,2},{4,5},{5,4},{6,7},{7,6},{8,9},{9,8},{10,11... | collective-permute-start | bytes 3145736 | tf_op jit(solution)/shard_map/ppermute | solution.py:72
  195.8 35.6 %collective-permute-start.59 = (bf16[256,2048]{1,0:T(8,128)(2,1)}, bf16[256,2048]{1,0:T(8,128)(2,1)}, u32[]{:S(2)}, u32[]{:S(2)}) collective-permute-start(bf16[256,2048]{1,0:T(8,128)(2,1)} %collective-permute-done.47.tokens_ref), channel_id=1, source_target_pairs={{0,16},{16,24},{24,8},{8,0},{1,17},{17,25},{25,9},{9,1},{2,18},{18... | collective-permute-start | bytes 3145736 | tf_op jit(solution)/shard_map/ppermute | solution.py:295
  205.5 14.0 %collective-permute-start.50 = (bf16[64,2048]{1,0:T(8,128)(2,1)}, bf16[64,2048]{1,0:T(8,128)(2,1)S(1)}, u32[]{:S(2)}, u32[]{:S(2)}) collective-permute-start(bf16[64,2048]{1,0:T(8,128)(2,1)} %get-tuple-element.114), channel_id=1, source_target_pairs={{0,4},{1,5},{2,6},{3,7},{4,0},{5,1},{6,2},{7,3},{8,12},{9,13},{10,... | collective-permute-start | bytes 786440 | tf_op jit(solution)/shard_map/ppermute | solution.py:72
  206.1 13.5 %collective-permute-start.51 = (bf16[64,2048]{1,0:T(8,128)(2,1)}, bf16[64,2048]{1,0:T(8,128)(2,1)S(1)}, u32[]{:S(2)}, u32[]{:S(2)}) collective-permute-start(bf16[64,2048]{1,0:T(8,128)(2,1)} %get-tuple-element.115), channel_id=1, source_target_pairs={{0,6},{1,7},{2,4},{3,5},{4,2},{5,3},{6,0},{7,1},{8,14},{9,15},{10,... | collective-permute-start | bytes 786440 | tf_op jit(solution)/shard_map/ppermute | solution.py:72
  231.5 27.8 %collective-permute-start.60 = (bf16[256,2048]{1,0:T(8,128)(2,1)}, bf16[256,2048]{1,0:T(8,128)(2,1)S(1)}, u32[]{:S(2)}, u32[]{:S(2)}) collective-permute-start(bf16[256,2048]{1,0:T(8,128)(2,1)} %collective-permute-done.59.tokens_ref), channel_id=1, source_target_pairs={{0,16},{16,24},{24,8},{8,0},{1,17},{17,25},{25,9},{9,1},{2,18},{18... | collective-permute-start | bytes 3145736 | tf_op jit(solution)/shard_map/ppermute | solution.py:295
  232.8 14.0 %collective-permute-start.63 = (bf16[64,2048]{1,0:T(8,128)(2,1)}, bf16[64,2048]{1,0:T(8,128)(2,1)S(1)}, u32[]{:S(2)}, u32[]{:S(2)}) collective-permute-start(bf16[64,2048]{1,0:T(8,128)(2,1)} %get-tuple-element.110), channel_id=1, source_target_pairs={{0,4},{1,5},{2,6},{3,7},{4,0},{5,1},{6,2},{7,3},{8,12},{9,13},{10,... | collective-permute-start | bytes 786440 | tf_op jit(solution)/shard_map/ppermute | solution.py:72
  259.3 27.2 %collective-permute-start.65 = (bf16[256,2048]{1,0:T(8,128)(2,1)S(1)}, bf16[256,2048]{1,0:T(8,128)(2,1)S(1)}, u32[]{:S(2)}, u32[]{:S(2)}) collective-permute-start(bf16[256,2048]{1,0:T(8,128)(2,1)S(1)} %collective-permute-done.60.tokens_ref), channel_id=1, source_target_pairs={{0,1},{1,0},{2,3},{3,2},{4,5},{5,4},{6,7},{7,6},{8,9},{9,8},{10,11... | collective-permute-start | bytes 3145736 | tf_op jit(solution)/shard_map/ppermute | solution.py:72
  260.6 14.2 %collective-permute-start.67 = (bf16[64,2048]{1,0:T(8,128)(2,1)}, bf16[64,2048]{1,0:T(8,128)(2,1)S(1)}, u32[]{:S(2)}, u32[]{:S(2)}) collective-permute-start(bf16[64,2048]{1,0:T(8,128)(2,1)} %get-tuple-element.130), channel_id=1, source_target_pairs={{0,4},{1,5},{2,6},{3,7},{4,0},{5,1},{6,2},{7,3},{8,12},{9,13},{10,... | collective-permute-start | bytes 786440 | tf_op jit(solution)/shard_map/ppermute | solution.py:72
  260.6 14.2 %collective-permute-start.68 = (bf16[64,2048]{1,0:T(8,128)(2,1)}, bf16[64,2048]{1,0:T(8,128)(2,1)S(1)}, u32[]{:S(2)}, u32[]{:S(2)}) collective-permute-start(bf16[64,2048]{1,0:T(8,128)(2,1)} %get-tuple-element.131), channel_id=1, source_target_pairs={{0,6},{1,7},{2,4},{3,5},{4,2},{5,3},{6,0},{7,1},{8,14},{9,15},{10,... | collective-permute-start | bytes 786440 | tf_op jit(solution)/shard_map/ppermute | solution.py:72
  281.3 43.0 %collective-permute-start.93 = (bf16[256,2048]{1,0:T(8,128)(2,1)}, bf16[256,2048]{1,0:T(8,128)(2,1)S(1)}, u32[]{:S(2)}, u32[]{:S(2)}) collective-permute-start(bf16[256,2048]{1,0:T(8,128)(2,1)} %weighed.4), channel_id=1, source_target_pairs={{0,16},{16,24},{24,8},{8,0},{1,17},{17,25},{25,9},{9,1},{2,18},{18... | collective-permute-start | bytes 3145736 | tf_op jit(solution)/shard_map/ppermute | solution.py:295
  283.9 13.7 %collective-permute-start.84 = (bf16[64,2048]{1,0:T(8,128)(2,1)}, bf16[64,2048]{1,0:T(8,128)(2,1)}, u32[]{:S(2)}, u32[]{:S(2)}) collective-permute-start(bf16[64,2048]{1,0:T(8,128)(2,1)} %get-tuple-element.123), channel_id=1, source_target_pairs={{0,4},{1,5},{2,6},{3,7},{4,0},{5,1},{6,2},{7,3},{8,12},{9,13},{10,... | collective-permute-start | bytes 786440 | tf_op jit(solution)/shard_map/ppermute | solution.py:72
  329.2 42.7 %collective-permute-start.94 = (bf16[256,2048]{1,0:T(8,128)(2,1)}, bf16[256,2048]{1,0:T(8,128)(2,1)S(1)}, u32[]{:S(2)}, u32[]{:S(2)}) collective-permute-start(bf16[256,2048]{1,0:T(8,128)(2,1)} %weighed.5), channel_id=1, source_target_pairs={{0,16},{16,24},{24,8},{8,0},{1,17},{17,25},{25,9},{9,1},{2,18},{18... | collective-permute-start | bytes 3145736 | tf_op jit(solution)/shard_map/ppermute | solution.py:295
  376.8 25.7 %collective-permute-start.95 = (bf16[256,2048]{1,0:T(8,128)(2,1)}, bf16[256,2048]{1,0:T(8,128)(2,1)S(1)}, u32[]{:S(2)}, u32[]{:S(2)}) collective-permute-start(bf16[256,2048]{1,0:T(8,128)(2,1)} %weighed.6), channel_id=1, source_target_pairs={{0,16},{16,24},{24,8},{8,0},{1,17},{17,25},{25,9},{9,1},{2,18},{18... | collective-permute-start | bytes 3145736 | tf_op jit(solution)/shard_map/ppermute | solution.py:295
  380.3 13.6 %collective-permute-start.53 = (bf16[64,2048]{1,0:T(8,128)(2,1)}, bf16[64,2048]{1,0:T(8,128)(2,1)S(1)}, u32[]{:S(2)}, u32[]{:S(2)}) collective-permute-start(bf16[64,2048]{1,0:T(8,128)(2,1)} %get-tuple-element.118), channel_id=1, source_target_pairs={{0,4},{1,5},{2,6},{3,7},{4,0},{5,1},{6,2},{7,3},{8,12},{9,13},{10,... | collective-permute-start | bytes 786440 | tf_op jit(solution)/shard_map/ppermute | solution.py:72
  (146 other events, 1463.5 us)
